TPU v7x, 32 devices: a whole 2x2x4 slice. The times are simulated.
32 devices in a mesh: ctx: 4 (over x, core), exp: 8 (over z, y).
Axes of the slice: x: 2, y: 2, z: 4, core: 2. Of those that a mesh axis runs over, the one named last changes fastest.
Arguments:
- q_nope: bfloat16 [128, 128, 512], P('ctx', 'exp'), may hold values from -72 to 72
- q_rope: bfloat16 [128, 8192], P('ctx', 'exp'), may hold values from -6 to 6
- cache_keys: bfloat16 [576, 512], P(None, 'ctx'), may hold values from -6 to 6
- fresh_keys: bfloat16 [576, 128], P(None, 'ctx'), may hold values from -6 to 6
- block_order: int32 [8], replicated, may hold values from 0 to 7, each once
- w_uv: bfloat16 [128, 512, 128], P('exp'), may hold values from -0.25 to 0.25
- w_out: bfloat16 [16384, 7168], P('exp', 'ctx'), may hold values from -0.046875 to 0.046875
- residual: bfloat16 [128, 7168], P(('ctx', 'exp')), may hold values from -6 to 6
- norm_gain: float32 [7168], replicated, may hold values from 0.5 to 1.5
- router_weight: bfloat16 [7168, 16], replicated, may hold values from -0.0625 to 0.0625
- expert_ids: int32 [128, 8], P(('ctx', 'exp')), may hold values from 0 to 15, all different within a row; in each aligned block of 4 rows (0 to 3, 4 to 7, ...) at most 3 rows name the same one
- w_gate: bfloat16 [16, 7168, 2048], P('exp', None, 'ctx'), may hold values from -0.0625 to 0.0625
- w_up: bfloat16 [16, 7168, 2048], P('exp', None, 'ctx'), may hold values from -0.0625 to 0.0625
- w_down: bfloat16 [16, 2048, 7168], P('exp', 'ctx'), may hold values from -0.125 to 0.125
Outputs:
- layer_out: bfloat16 [128, 7168], P(('ctx', 'exp'))
Inputs may be any that keep to these rules, and one draw needn't show every extreme that they name: A permutation: block j of the new tokens (16 rows) sits at positions 512 + block_order[j] * 16 onward. `expert_ids`: each row names 8 different experts; the 4 rows of one device name no expert more than 3 times, and in some aligned block one expert exactly 3 times.
All inputs are finite; a program needn't handle non-finite values.
Results may differ from a plain program's by a relative error of at most 0.012.
Values may be sent and summed in bfloat16 or wider, within the bound.
A program may use at most 128 MiB of HBM per device.

v0:
```python
import math

import jax
import jax.numpy as jnp
from jax import lax
from jax.sharding import PartitionSpec as P

QKD = 192
CAP = 3


ROUTE_SCALE = 2.5
NORM_EPS = 1e-06


def block_position(row_index, block_order, block_rows):
    blocks = row_index // block_rows
    lookup = blocks[:, None] == jnp.arange(block_order.shape[0], dtype=jnp.int32)[None, :]
    leading = jnp.sum(jnp.where(lookup, block_order[None, :], 0), axis=1)
    return leading * block_rows + row_index % block_rows


def attend(query_lat, query_pe, keys, visible):
    row_count, head_count, latent_width = query_lat.shape
    key_count = keys.shape[1]
    pe_width = query_pe.shape[1] // head_count
    first_dot = jnp.dot(
        query_lat.reshape(row_count * head_count, latent_width),
        keys[:latent_width],
        preferred_element_type=jnp.float32,
    )
    second_dot = jnp.dot(
        query_pe.reshape(row_count * head_count, pe_width),
        keys[latent_width:],
        preferred_element_type=jnp.float32,
    )
    scores = ((first_dot + second_dot) * (1.0 / math.sqrt(QKD))).reshape(
        row_count, head_count, key_count
    )
    scores = jnp.where(visible[:, None, :], scores, -jnp.inf)
    row_max = jnp.max(scores, axis=2)
    exponent = jnp.exp(scores - row_max[:, :, None])
    row_sum = jnp.sum(exponent, axis=2)
    weights = exponent.astype(jnp.bfloat16).reshape(row_count * head_count, key_count)
    latent = lax.dot_general(
        weights, keys[:latent_width], (((1,), (1,)), ((), ())), preferred_element_type=jnp.float32
    )
    return (row_max, row_sum, latent.reshape(row_count, head_count, latent_width))


def merge_partial(earlier, latter):
    highest = latter[0]
    earlier_scale = jnp.exp(earlier[0] - highest)
    latter_scale = jnp.exp(latter[0] - highest)
    row_sum = earlier_scale * earlier[1] + latter_scale * latter[1]
    latent = earlier_scale[:, :, None] * earlier[2] + latter_scale[:, :, None] * latter[2]
    return (highest, row_sum, latent)


def body(
    q_nope,
    q_rope,
    cache_keys,
    fresh_keys,
    block_order,
    w_uv,
    w_out,
    residual,
    norm_gain,
    router_weight,
    expert_ids,
    w_gate,
    w_up,
    w_down,
):
    ctx_count = lax.axis_size("ctx")
    exp_count = lax.axis_size("exp")
    ctx_index = lax.axis_index("ctx")
    rows_here, heads_here, latent_width = q_nope.shape
    value_width = w_uv.shape[2]
    cache_len = cache_keys.shape[1]
    key_cols = cache_len + rows_here
    block_rows = rows_here // 2
    keys_here = jnp.concatenate([cache_keys, fresh_keys], axis=1)
    w_uv_wide = w_uv.astype(jnp.float32)
    own_rows = ctx_index * rows_here + jnp.arange(rows_here, dtype=jnp.int32)
    own_pos = block_position(own_rows, block_order, block_rows)
    start_state = (
        jnp.full((rows_here, heads_here), -jnp.inf, jnp.float32),
        jnp.zeros((rows_here, heads_here), jnp.float32),
        jnp.zeros((rows_here, heads_here, latent_width), jnp.float32),
    )
    portion = lax.all_gather(keys_here, "ctx", axis=1, tiled=True)
    columns = jnp.arange(portion.shape[1], dtype=jnp.int32)
    owner_dev = columns // key_cols
    within = columns % key_cols
    fresh_row = owner_dev * rows_here + within - cache_len
    key_pos = jnp.where(within < cache_len, -1, block_position(fresh_row, block_order, block_rows))
    visible = key_pos[None, :] <= own_pos[:, None]
    row_max, row_sum, latent = merge_partial(start_state, attend(q_nope, q_rope, portion, visible))
    normal_lat = latent / row_sum[:, :, None]
    head_wide = jnp.einsum("rhl,hlv->rhv", normal_lat, w_uv_wide, precision=lax.Precision.HIGHEST)
    head_out = head_wide.astype(jnp.bfloat16).reshape(rows_here, heads_here * value_width)
    tok_here, model_width = residual.shape
    col_part = w_out.shape[1]
    head_partial = jnp.dot(
        lax.all_gather(head_out, "ctx", axis=0, tiled=True),
        w_out,
        preferred_element_type=jnp.float32,
    )
    arranged = head_partial.reshape(ctx_count, exp_count, tok_here, col_part)
    head_total = lax.psum_scatter(
        arranged.astype(jnp.bfloat16), "exp", scatter_dimension=1, tiled=True
    )
    attention = lax.all_to_all(head_total, "ctx", split_axis=0, concat_axis=3, tiled=True).reshape(
        tok_here, model_width
    )
    hidden = residual.astype(jnp.float32) + attention.astype(jnp.float32)
    mean_square = jnp.mean(hidden * hidden, axis=1, keepdims=True)
    normed = (hidden * lax.rsqrt(mean_square + NORM_EPS) * norm_gain).astype(jnp.bfloat16)
    affinity = jax.nn.sigmoid(jnp.dot(normed, router_weight, preferred_element_type=jnp.float32))
    expert_count = router_weight.shape[1]
    onehot = expert_ids[:, :, None] == jnp.arange(expert_count, dtype=jnp.int32)[None, None, :]
    chosen = jnp.sum(jnp.where(onehot, affinity[:, None, :], 0.0), axis=2)
    route = ROUTE_SCALE * chosen / jnp.sum(chosen, axis=1, keepdims=True)
    mixing = jnp.sum(jnp.where(onehot, route[:, :, None], 0.0), axis=1)
    picked = jnp.sum(onehot.astype(jnp.int32), axis=1)
    slot_index = jnp.cumsum(picked, axis=0) - picked
    slot_hot = (slot_index[:, :, None] == jnp.arange(CAP, dtype=jnp.int32)[None, None, :]) & (
        picked[:, :, None] > 0
    )
    dispatch_map = (
        jnp.transpose(slot_hot, (1, 2, 0))
        .reshape(expert_count * CAP, tok_here)
        .astype(jnp.bfloat16)
    )
    send_rows = jnp.dot(dispatch_map, normed, preferred_element_type=jnp.float32).astype(
        jnp.bfloat16
    )
    arrived = lax.all_to_all(
        send_rows.reshape(expert_count, CAP, model_width),
        "exp",
        split_axis=0,
        concat_axis=1,
        tiled=True,
    )
    local_experts = arrived.shape[0]
    portion = lax.all_gather(arrived, "ctx", axis=1, tiled=True)
    gate = jnp.einsum("end,edf->enf", portion, w_gate, preferred_element_type=jnp.float32)
    upward = jnp.einsum("end,edf->enf", portion, w_up, preferred_element_type=jnp.float32)
    activations = (jax.nn.silu(gate) * upward).astype(jnp.bfloat16)
    expert_total = lax.psum_scatter(
        jnp.einsum("enf,efd->ned", activations, w_down, preferred_element_type=jnp.float32).astype(
            jnp.bfloat16
        ),
        "ctx",
        scatter_dimension=0,
        tiled=True,
    )
    going_back = expert_total.reshape(exp_count, CAP, local_experts, model_width)
    returned = lax.all_to_all(going_back, "exp", split_axis=0, concat_axis=2, tiled=True)
    combine_map = jnp.where(slot_hot, mixing[:, :, None], 0.0)
    combine_map = jnp.transpose(combine_map, (0, 2, 1)).reshape(tok_here, CAP * expert_count)
    mixture = jnp.dot(
        combine_map,
        returned.reshape(CAP * expert_count, model_width).astype(jnp.float32),
        precision=lax.Precision.HIGHEST,
    )
    return (hidden + mixture).astype(jnp.bfloat16)


def solution(mesh):
    return jax.shard_map(
        body,
        mesh=mesh,
        in_specs=(
            P("ctx", "exp", None),
            P("ctx", "exp"),
            P(None, "ctx"),
            P(None, "ctx"),
            P(),
            P("exp", None, None),
            P("exp", "ctx"),
            P(("ctx", "exp"), None),
            P(),
            P(),
            P(("ctx", "exp"), None),
            P("exp", None, "ctx"),
            P("exp", None, "ctx"),
            P("exp", "ctx", None),
        ),
        out_specs=P(("ctx", "exp"), None),
        check_vma=False,
    )
```

profile of v0, /device:TPU:0, one launch (start us, length us, event | category | flops | bytes accessed | tf_op | source)
XLA Modules:
  0.0 268.8 jit_solution(8497776579315052715)
XLA Ops:
  6.6 0.9 select_reduce_fusion.4
  7.5 0.7 select_reduce_fusion.2
  8.2 1.0 reshape.299
  9.2 1.1 copy.39
  10.3 0.8 pad_maximum_fusion
  11.1 10.3 %all_gather.9 = bf16[576,640]{0,1:T(8,128)(2,1)S(1)} all-gather(bf16[576,160]{0,1:T(8,128)(2,1)S(1)} %pad_maximum_fusion), channel_id=1, replica_groups=mesh['ctx'=4,'exp'=8] {'ctx'}, dimensions={1}, use_global_device_ids=true | all-gather | bytes 921600 | tf_op jit(solution)/shard_map/all_gather | solution.py:93
  21.4 1.6 fusion.16
  23.1 0.1 broadcast_in_dim.113
  23.2 0.5 fusion.39
  23.7 1.1 fusion.8
  25.3 1.7 fusion.6
  27.0 1.0 fusion.10
  28.1 7.3 %all_gather.10 = bf16[128,2048]{1,0:T(8,128)(2,1)S(1)} all-gather(bf16[32,2048]{1,0:T(8,128)(2,1)S(1)} %bitcast.75), channel_id=1, replica_groups=mesh['ctx'=4,'exp'=8] {'ctx'}, dimensions={0}, use_global_device_ids=true | all-gather | bytes 655360 | tf_op jit(solution)/shard_map/all_gather | solution.py:107
  35.3 4.2 %convolution_convert_fusion.2 = bf16[128,1792]{1,0:T(8,128)(2,1)S(1)} fusion(bf16[128,2048]{1,0:T(8,128)(2,1)S(1)} %all_gather.10, bf16[2048,1792]{1,0:T(8,128)(2,1)} %param.20), kind=kOutput, calls=%fused_computation.5 | convolution fusion | flops 939753472 | bytes 8323072 | tf_op jit(solution)/shard_map/dot_general | solution.py:106
  39.6 0.9 convert_element_type.60
  40.5 0.6 dynamic-slice
  41.1 0.1 convert_reduce_fusion
  41.2 72.6 %all-reduce.3.cloned.1.call-done = bf16[4,8,4,1792]{3,2,1,0:T(4,128)(2,1)} async-done(((bf16[4,8,4,1792]{3,2,1,0:T(4,128)(2,1)}), bf16[4,8,4,1792]{3,2,1,0:T(4,128)(2,1)}) %all-reduce.3.cloned.1.call-update) | async-done | bytes 458768
  113.9 2.1 constant_dynamic-slice_fusion
  115.9 3.3 %all-to-all-start = ((bf16[4,1,4,1792]{3,2,1,0:T(4,128)(2,1)}), bf16[4,1,4,1792]{3,2,1,0:T(4,128)(2,1)S(1)}, u32[]{:S(2)}, u32[]{:S(2)}) async-start(bf16[4,1,4,1792]{3,2,1,0:T(4,128)(2,1)} %constant_dynamic-slice_fusion), calls=%async_computation | async-start | bytes 114688 | tf_op jit(solution)/shard_map/all_to_all | solution.py:115
  119.4 0.1 and.113
  119.5 0.1 eq.95
  119.7 0.1 eq.93
  119.8 3.5 %all-to-all-done = bf16[4,1,4,1792]{3,2,1,0:T(4,128)(2,1)S(1)} async-done(((bf16[4,1,4,1792]{3,2,1,0:T(4,128)(2,1)}), bf16[4,1,4,1792]{3,2,1,0:T(4,128)(2,1)S(1)}, u32[]{:S(2)}, u32[]{:S(2)}) %all-to-all-start) | async-done | bytes 57376 | tf_op jit(solution)/shard_map/all_to_all | solution.py:115
  123.3 0.2 multiply_reduce_fusion
  123.5 0.1 multiply_convert_fusion
  123.6 0.3 copy-done.3
  123.9 0.4 convolution_convert_fusion.1
  124.3 0.4 reshape.301
  124.8 26.9 %all_to_all.42 = bf16[16,3,7168]{2,1,0:T(4,128)(2,1)S(1)} all-to-all(bf16[16,3,7168]{2,1,0:T(4,128)(2,1)S(1)} %reshape.301), channel_id=1, replica_groups=mesh['ctx'=4,'exp'=8] {'exp'}, dimensions={0} | all-to-all | bytes 1376256 | tf_op jit(solution)/shard_map/all_to_all | solution.py:140
  151.6 0.6 copy.46
  152.2 1.0 copy.47
  153.2 0.2 reduce-scatter.5.cloned.1.call-start
  153.5 23.9 %all-gather.2.cloned.1.call-done = bf16[2,96,7168]{2,1,0:T(8,128)(2,1)} async-done(((bf16[2,24,7168]{2,1,0:T(8,128)(2,1)}), bf16[2,96,7168]{2,1,0:T(8,128)(2,1)}) %all-gather.2.cloned.1.call-update) | async-done | bytes 2752528 | tf_op jit(solution)/shard_map/all_gather | solution.py:148
  177.4 8.6 %fusion.40 = f32[2,96,512]{2,1,0:T(8,128)S(1)} fusion(bf16[2,96,7168]{2,1,0:T(8,128)(2,1)} %all-gather.2.cloned.1.call-done, bf16[2,7168,512]{2,1,0:T(8,128)(2,1)} %param.25), kind=kOutput, calls=%fused_computation.91 | convolution fusion | flops 1409286144 | bytes 17825792 | tf_op jit(solution)/shard_map/end,edf->enf/dot_general | solution.py:149
  186.0 7.8 %fusion.7 = bf16[2,96,512]{2,1,0:T(8,128)(2,1)S(1)} fusion(bf16[2,96,7168]{2,1,0:T(8,128)(2,1)S(1)} %copy-done.2, bf16[2,7168,512]{2,1,0:T(8,128)(2,1)} %param.26, f32[2,96,512]{2,1,0:T(8,128)S(1)} %fusion.40), kind=kOutput, calls=%fused_computation.15 | convolution fusion | flops 1409875968 | bytes 18022400 | tf_op jit(solution)/shard_map/end,edf->enf/dot_general | solution.py:150
  193.8 2.6 fusion
  196.4 1.8 copy.56
  198.2 35.5 %reduce-scatter.5.cloned.1.call-done = bf16[24,14336]{1,0:T(8,128)(2,1)} async-done(((bf16[96,14336]{1,0:T(8,128)(2,1)}), bf16[24,14336]{1,0:T(8,128)(2,1)}) %reduce-scatter.5.cloned.1.call-update) | async-done | bytes 688144
  233.7 2.6 reshape.310
  236.3 5.5 %all-to-all-start.2 = ((bf16[8,3,2,7168]{3,2,1,0:T(2,128)(2,1)}), bf16[8,3,2,7168]{3,2,1,0:T(2,128)(2,1)S(1)}, u32[]{:S(2)}, u32[]{:S(2)}) async-start(bf16[8,3,2,7168]{3,2,1,0:T(2,128)(2,1)} %bitcast.15), calls=%async_computation.2 | async-start | bytes 1376256 | tf_op jit(solution)/shard_map/all_to_all | solution.py:161
  241.8 0.2 fusion.13
  242.0 0.2 select_reduce_fusion
  242.3 0.1 select_reduce_fusion.3
  242.5 17.2 %all-to-all-done.2 = bf16[8,3,2,7168]{3,2,1,0:T(2,128)(2,1)S(1)} async-done(((bf16[8,3,2,7168]{3,2,1,0:T(2,128)(2,1)}), bf16[8,3,2,7168]{3,2,1,0:T(2,128)(2,1)S(1)}, u32[]{:S(2)}, u32[]{:S(2)}) %all-to-all-start.2) | async-done | bytes 688160 | tf_op jit(solution)/shard_map/all_to_all | solution.py:161
  259.7 0.5 copy.49
  260.1 0.3 reshape.303
  260.4 1.9 fusion.1
  (57 shorter events, 1.2 us)
Async XLA Ops:
  6.5 20.5 %copy-start = (bf16[16,512,128]{2,1,0:T(8,128)(2,1)S(1)}, bf16[16,512,128]{2,1,0:T(8,128)(2,1)}, u32[]{:S(2)}) copy-start(bf16[16,512,128]{2,1,0:T(8,128)(2,1)} %param.19) | copy-start | bytes 6291460
  6.5 107.3 %all-reduce.3.cloned.1.call-start = ((), (), s32[]{:S(2)}) async-start(), calls=%async_computation.6 | async-start | bytes 917504
  35.3 5.2 %copy-start.8 = (u32[32]{0:T(128)S(1)}, u32[32]{0:T(128)}, u32[]{:S(2)}) copy-start(u32[32]{0:T(128)} %constant.104) | copy-start | bytes 388
  35.3 5.8 %copy-start.6 = (s32[4,8]{1,0:T(4,128)S(1)}, s32[4,8]{1,0:T(4,128)}, u32[]{:S(2)}) copy-start(s32[4,8]{1,0:T(4,128)} %param.24) | copy-start | bytes 388
  35.3 87.9 %copy-start.4 = (bf16[4,7168]{1,0:T(4,128)(2,1)S(1)}, bf16[4,7168]{1,0:T(4,128)(2,1)}, u32[]{:S(2)}) copy-start(bf16[4,7168]{1,0:T(4,128)(2,1)} %param.21) | copy-start | bytes 172036
  35.3 88.1 %copy-start.5 = (f32[7168]{0:T(1024)S(1)}, f32[7168]{0:T(1024)}, u32[]{:S(2)}) copy-start(f32[7168]{0:T(1024)} %param.22) | copy-start | bytes 86020
  115.9 7.3 %all-to-all-start = ((bf16[4,1,4,1792]{3,2,1,0:T(4,128)(2,1)}), bf16[4,1,4,1792]{3,2,1,0:T(4,128)(2,1)S(1)}, u32[]{:S(2)}, u32[]{:S(2)}) async-start(bf16[4,1,4,1792]{3,2,1,0:T(4,128)(2,1)} %constant_dynamic-slice_fusion), calls=%async_computation | async-start | bytes 114688 | tf_op jit(solution)/shard_map/all_to_all | solution.py:115
  119.2 58.2 %all-gather.2.cloned.1.call-start = ((), (), s32[]{:S(2)}) async-start(), calls=%async_computation.4 | async-start | bytes 3440640 | tf_op jit(solution)/shard_map/all_gather | solution.py:148
  123.3 0.7 copy-start.3
  153.2 80.5 %reduce-scatter.5.cloned.1.call-start = ((), (), s32[]{:S(2)}) async-start(), calls=%async_computation.5 | async-start | bytes 3440640
  177.4 8.6 %copy-start.2 = (bf16[2,96,7168]{2,1,0:T(8,128)(2,1)S(1)}, bf16[2,96,7168]{2,1,0:T(8,128)(2,1)}, u32[]{:S(2)}) copy-start(bf16[2,96,7168]{2,1,0:T(8,128)(2,1)} %all-gather.2.cloned.1.call-done) | copy-start | bytes 8257540
  177.4 16.4 %slice-start = ((s8[14680064]{0:T(1024)(128)(4,1)}), s8[4194304]{0:T(1024)(128)(4,1)S(1)}, s32[]{:S(2)}) async-start(s8[14680064]{0:T(1024)(128)(4,1)} %bitcast.63), calls=%async_computation.7 | async-start | bytes 8388608
  177.4 16.4 %slice-start.1 = ((s8[14680064]{0:T(1024)(128)(4,1)}), s8[4194304]{0:T(1024)(128)(4,1)S(1)}, s32[]{:S(2)}) async-start(s8[14680064]{0:T(1024)(128)(4,1)} %bitcast.63), calls=%async_computation.8 | async-start | bytes 8388608
  186.0 7.8 %slice-start.2 = ((s8[14680064]{0:T(1024)(128)(4,1)}), s8[4194304]{0:T(1024)(128)(4,1)S(1)}, s32[]{:S(2)}) async-start(s8[14680064]{0:T(1024)(128)(4,1)} %bitcast.63), calls=%async_computation.9 | async-start | bytes 8388608
  186.0 7.8 %slice-start.3 = ((s8[14680064]{0:T(1024)(128)(4,1)}), s8[2097152]{0:T(1024)(128)(4,1)S(1)}, s32[]{:S(2)}) async-start(s8[14680064]{0:T(1024)(128)(4,1)} %bitcast.63), calls=%async_computation.10 | async-start | bytes 4194304
  198.2 43.6 %copy-start.7 = (bf16[7168,16]{0,1:T(8,128)(2,1)S(1)}, bf16[7168,16]{0,1:T(8,128)(2,1)}, u32[]{:S(2)}) copy-start(bf16[7168,16]{0,1:T(8,128)(2,1)} %param.23) | copy-start | bytes 688132
  233.7 28.6 %copy-start.1 = (bf16[16,512,128]{2,1,0:T(8,128)(2,1)S(1)}, bf16[16,512,128]{2,1,0:T(8,128)(2,1)}, u32[]{:S(2)}) copy-start(bf16[16,512,128]{2,1,0:T(8,128)(2,1)} %param.19) | copy-start | bytes 6291460
  236.3 23.4 %all-to-all-start.2 = ((bf16[8,3,2,7168]{3,2,1,0:T(2,128)(2,1)}), bf16[8,3,2,7168]{3,2,1,0:T(2,128)(2,1)S(1)}, u32[]{:S(2)}, u32[]{:S(2)}) async-start(bf16[8,3,2,7168]{3,2,1,0:T(2,128)(2,1)} %bitcast.15), calls=%async_computation.2 | async-start | bytes 1376256 | tf_op jit(solution)/shard_map/all_to_all | solution.py:161
Sparse Core Ops, SparseCore 0:
  40.6 73.1 all-reduce.2
  153.3 23.9 all-gather.1
  198.3 35.3 reduce-scatter.4
where the time goes:
time: 270 us; the launch traced here: 269 us
  waiting for transfers between devices  153 us (57%)
  blocking collectives  44.4 us (16%)
  matrix products  30.6 us (11%)
  local copies, waits for them, and re-layouts  14.2 us (5%)
  between operations  13.4 us (5%)
  starting transfers between devices  9.06 us (3%)
  other arithmetic  4.49 us (2%)
    unnamed x5, waiting for transfers between devices  108 us
    all_to_all x1, blocking collectives, body(): lax.all_to_all(send_rows.reshape(expert_count, CAP, model_width), 'exp',...  26.9 us
    all_gather x1, waiting for transfers between devices, body(): portion = lax.all_gather(arrived, 'ctx', axis=1, tiled=True)  23.9 us
    all_to_all x1, waiting for transfers between devices, body(): lax.all_to_all(going_back, 'exp', split_axis=0, concat_axis=2, tiled=True)  17.2 us
    all_gather x1, blocking collectives, body(): portion = lax.all_gather(keys_here, 'ctx', axis=1, tiled=True)  10.3 us
    dot_general x1, matrix products, body(): jnp.einsum('end,edf->enf', portion, w_gate, preferred_element_type=jnp.fl...  8.57 us
    dot_general x1, matrix products, body(): jnp.einsum('end,edf->enf', portion, w_up, preferred_element_type=jnp.floa...  7.8 us
    all_gather x1, blocking collectives, body(): lax.all_gather(head_out, 'ctx', axis=0, tiled=True)  7.27 us
  transfers between devices with their start and end apart: 5, of which 5 were waited for; matrix products, arithmetic and copies ran while one was open for 1% of the time, Pallas kernels for 0%

commit v1 on v0

v1 whole, which is shorter than its diff:
```python
import functools
import math

import jax
import jax.numpy as jnp
from jax import lax
from jax.experimental import pallas as pl
from jax.experimental.pallas import tpu as pltpu
from jax.sharding import PartitionSpec as P

QKD = 192
VMEM_BYTES = 48 * 1024 * 1024

ROUTE_SCALE = 2.5
NORM_EPS = 1e-06


def block_position(row_index, block_order, block_rows):
    blocks = row_index // block_rows
    lookup = blocks[:, None] == jnp.arange(block_order.shape[0], dtype=jnp.int32)[None, :]
    leading = jnp.sum(jnp.where(lookup, block_order[None, :], 0), axis=1)
    return leading * block_rows + row_index % block_rows


def attend(query_lat, query_pe, keys, visible):
    row_count, head_count, latent_width = query_lat.shape
    key_count = keys.shape[1]
    pe_width = query_pe.shape[1] // head_count
    first_dot = jnp.dot(
        query_lat.reshape(row_count * head_count, latent_width),
        keys[:latent_width],
        preferred_element_type=jnp.float32,
    )
    second_dot = jnp.dot(
        query_pe.reshape(row_count * head_count, pe_width),
        keys[latent_width:],
        preferred_element_type=jnp.float32,
    )
    scores = ((first_dot + second_dot) * (1.0 / math.sqrt(QKD))).reshape(
        row_count, head_count, key_count
    )
    scores = jnp.where(visible[:, None, :], scores, -jnp.inf)
    row_max = jnp.max(scores, axis=2)
    exponent = jnp.exp(scores - row_max[:, :, None])
    row_sum = jnp.sum(exponent, axis=2)
    weights = exponent.astype(jnp.bfloat16).reshape(row_count * head_count, key_count)
    latent = lax.dot_general(
        weights, keys[:latent_width], (((1,), (1,)), ((), ())), preferred_element_type=jnp.float32
    )
    return (row_max, row_sum, latent.reshape(row_count, head_count, latent_width))


def remote(src, dst, send, recv, target):
    return pltpu.make_async_remote_copy(
        src_ref=src,
        dst_ref=dst,
        send_sem=send,
        recv_sem=recv,
        device_id=target,
        device_id_type=pl.DeviceIdType.MESH,
    )


def place():
    ctx_count, exp_count = lax.axis_size("ctx"), lax.axis_size("exp")
    ctx, exp = lax.axis_index("ctx"), lax.axis_index("exp")
    return ctx_count // 2, exp_count, ctx, exp, ctx // 2, ctx % 2


def start_gather(src, out, send, recv):
    chips, _, ctx, exp, chip, core = place()
    flights = []
    for k in range(chips):
        peer = ctx + 1 - 2 * core if k == 0 else (chip + k) % chips * 2 + core
        copy = remote(src, out.at[ctx], send.at[0, k], recv.at[0, k], (peer, exp))
        copy.start()
        flights.append(copy)
    return flights


def finish_gather(out, flights, send, recv):
    chips, _, ctx, exp, chip, core = place()
    relayed = []
    for k in range(1, chips):
        flights[k].wait_recv()
        origin = (chip + chips - k) % chips * 2 + core
        copy = remote(
            out.at[origin], out.at[origin], send.at[1, k], recv.at[1, k], (ctx + 1 - 2 * core, exp)
        )
        copy.start()
        relayed.append(copy)
    flights[0].wait_recv()
    for copy in relayed:
        copy.wait_recv()
    for copy in flights + relayed:
        copy.wait_send()


def inputs_kernel(
    cache, fresh, res, ids, cache_out, fresh_out, res_out, ids_out,
    c_send, c_recv, f_send, f_recv, r_send, r_recv, i_send, i_recv, j_send, j_recv,
):
    chips, exp_count, ctx, exp, chip, core = place()
    ctx_count = 2 * chips
    id_flights = []
    for k in range(1, exp_count):
        copy = remote(
            ids, ids_out.at[ctx, exp], i_send.at[k], i_recv.at[k], (ctx, (exp + k) % exp_count)
        )
        copy.start()
        id_flights.append(copy)
    cache_flights = start_gather(cache, cache_out, c_send, c_recv)
    fresh_flights = start_gather(fresh, fresh_out, f_send, f_recv)
    res_flights = []
    for k in range(1, ctx_count):
        peer = (ctx + k) % ctx_count
        copy = remote(res.at[peer], res_out.at[ctx], r_send.at[k], r_recv.at[k], (peer, exp))
        copy.start()
        res_flights.append(copy)
    cache_out[ctx] = cache[...]
    fresh_out[ctx] = fresh[...]
    res_out[ctx] = res[ctx]
    ids_out[ctx, exp] = ids[...]
    for copy in id_flights:
        copy.wait()
    for k in range(1, ctx_count):
        copy = remote(
            ids_out.at[ctx],
            ids_out.at[ctx],
            j_send.at[k],
            j_recv.at[k],
            ((ctx + k) % ctx_count, exp),
        )
        copy.start()
        res_flights.append(copy)
    finish_gather(cache_out, cache_flights, c_send, c_recv)
    finish_gather(fresh_out, fresh_flights, f_send, f_recv)
    for copy in res_flights:
        copy.wait()


def heads_kernel(src, out, send, recv):
    _, _, ctx, _, _, _ = place()
    flights = start_gather(src, out, send, recv)
    out[ctx] = src[...]
    finish_gather(out, flights, send, recv)


def hidden_kernel(
    part, res, out, landed, a_send, a_recv, b_send, b_recv, x_send, x_recv, f_send, f_recv
):
    chips, exp_count, ctx, exp, chip, core = place()
    partner = ctx + 1 - 2 * core
    first = []
    for k in range(1, exp_count):
        peer = (exp + k) % exp_count
        copy = remote(part.at[peer], landed.at[k], a_send.at[k], a_recv.at[k], (ctx, peer))
        copy.start()
        first.append(copy)
    total = part[exp].astype(jnp.float32)
    for k in range(1, exp_count):
        first[k - 1].wait_recv()
        total = total + landed[k].astype(jnp.float32)
    out[ctx, exp] = (res[...].astype(jnp.float32) + total).astype(jnp.bfloat16)
    pending = []
    spread = [None]
    for k in range(1, exp_count):
        copy = remote(
            out.at[ctx, exp],
            out.at[ctx, exp],
            b_send.at[k],
            b_recv.at[k],
            (ctx, (exp + k) % exp_count),
        )
        copy.start()
        spread.append(copy)
    for k in range(exp_count):
        if k > 0:
            spread[k].wait_recv()
        source = (exp + exp_count - k) % exp_count
        block = out.at[ctx, source]
        row = []
        for p in range(chips):
            peer = partner if p == 0 else (chip + p) % chips * 2 + core
            copy = remote(block, block, x_send.at[p, k], x_recv.at[p, k], (peer, exp))
            copy.start()
            row.append(copy)
        pending.append(row)
    last = []
    for k in range(exp_count):
        source = (exp + exp_count - k) % exp_count
        for p in range(1, chips):
            pending[k][p].wait_recv()
            origin = (chip + chips - p) % chips * 2 + core
            block = out.at[origin, source]
            copy = remote(block, block, f_send.at[p, k], f_recv.at[p, k], (partner, exp))
            copy.start()
            last.append(copy)
    for row in pending:
        row[0].wait_recv()
    for copy in last:
        copy.wait()
    for copy in first + spread[1:] + [copy for row in pending for copy in row]:
        copy.wait_send()


def combine_kernel(
    y, hid, out, pair, cross_out, cross_in, home_out, home_in,
    p_send, p_recv, x_send, x_recv, e_send, e_recv,
):
    chips, exp_count, ctx, exp, chip, core = place()
    partner = ctx + 1 - 2 * core
    order = list(range(1, exp_count)) + [0]
    halves, crossing, homing = {}, {}, {}
    for k in order:
        dest = (exp + k) % exp_count
        for j in list(range(1, chips)) + [0]:
            theirs = (chip + j) % chips * 2 + 1 - core
            copy = remote(
                y.at[dest, theirs], pair.at[k, j], p_send.at[k, j], p_recv.at[k, j], (partner, exp)
            )
            copy.start()
            halves[k, j] = copy
    for k in order:
        dest = (exp + k) % exp_count
        for j in range(1, chips):
            owner = (chip + j) % chips * 2 + core
            halves[k, j].wait_recv()
            both = y[dest, owner].astype(jnp.float32) + pair[k, j].astype(jnp.float32)
            cross_out[k, j] = both.astype(jnp.bfloat16)
            copy = remote(
                cross_out.at[k, j],
                cross_in.at[k, j],
                x_send.at[k, j],
                x_recv.at[k, j],
                (owner, exp),
            )
            copy.start()
            crossing[k, j] = copy
    total = hid[...].astype(jnp.float32)
    for k in order:
        dest = (exp + k) % exp_count
        halves[k, 0].wait_recv()
        both = y[dest, ctx].astype(jnp.float32) + pair[k, 0].astype(jnp.float32)
        for j in range(1, chips):
            crossing[k, j].wait_recv()
            both = both + cross_in[k, j].astype(jnp.float32)
        if k == 0:
            total = total + both
        else:
            home_out[k] = both.astype(jnp.bfloat16)
            copy = remote(
                home_out.at[k], home_in.at[k], e_send.at[k], e_recv.at[k], (ctx, dest)
            )
            copy.start()
            homing[k] = copy
    for k in range(1, exp_count):
        homing[k].wait_recv()
        total = total + home_in[k].astype(jnp.float32)
    out[...] = total.astype(jnp.bfloat16)
    for copy in list(halves.values()) + list(crossing.values()) + list(homing.values()):
        copy.wait_send()


def exchange(kernel, shapes, scratch, *operands):
    vmem = pl.BlockSpec(memory_space=pltpu.VMEM)
    return pl.pallas_call(
        kernel,
        out_shape=shapes,
        in_specs=[vmem] * len(operands),
        out_specs=jax.tree.map(lambda _: vmem, shapes),
        scratch_shapes=scratch,
        compiler_params=pltpu.CompilerParams(
            has_side_effects=True, vmem_limit_bytes=VMEM_BYTES
        ),
    )(*operands)


def body(
    q_nope,
    q_rope,
    cache_keys,
    fresh_keys,
    block_order,
    w_uv,
    w_out,
    residual,
    norm_gain,
    router_weight,
    expert_ids,
    w_gate,
    w_up,
    w_down,
):
    ctx_count = lax.axis_size("ctx")
    exp_count = lax.axis_size("exp")
    ctx_index = lax.axis_index("ctx")
    exp_index = lax.axis_index("exp")
    rows_here, heads_here, latent_width = q_nope.shape
    value_width = w_uv.shape[2]
    key_width, cache_len = cache_keys.shape
    tok_here, model_width = residual.shape
    col_part = w_out.shape[1]
    chips = ctx_count // 2
    block_rows = rows_here * ctx_count // block_order.shape[0]
    dma = pltpu.SemaphoreType.DMA
    bf16 = functools.partial(jax.ShapeDtypeStruct, dtype=jnp.bfloat16)

    res_cols = residual.reshape(tok_here, ctx_count, col_part).transpose(1, 0, 2)
    cache_all, fresh_all, res_own, ids_all = exchange(
        inputs_kernel,
        (
            bf16((ctx_count, key_width, cache_len)),
            bf16((ctx_count, rows_here, key_width)),
            bf16((ctx_count, tok_here, col_part)),
            jax.ShapeDtypeStruct((ctx_count, exp_count) + expert_ids.shape, jnp.int32),
        ),
        [dma((2, chips))] * 4 + [dma((ctx_count,))] * 2 + [dma((exp_count,))] * 2
        + [dma((ctx_count,))] * 2,
        cache_keys, fresh_keys.T, res_cols, expert_ids,
    )
    cached = jnp.transpose(cache_all, (1, 0, 2)).reshape(key_width, ctx_count * cache_len)
    fresh = fresh_all.reshape(ctx_count * rows_here, key_width).T
    keys = jnp.concatenate([cached, fresh], axis=1)
    own_rows = ctx_index * rows_here + jnp.arange(rows_here, dtype=jnp.int32)
    own_pos = block_position(own_rows, block_order, block_rows)
    new_rows = jnp.arange(ctx_count * rows_here, dtype=jnp.int32)
    key_pos = jnp.concatenate(
        [
            jnp.full((ctx_count * cache_len,), -1, jnp.int32),
            block_position(new_rows, block_order, block_rows),
        ]
    )
    visible = key_pos[None, :] <= own_pos[:, None]
    row_max, row_sum, latent = attend(q_nope, q_rope, keys, visible)
    normal_lat = (latent / row_sum[:, :, None]).astype(jnp.bfloat16)
    head_out = jnp.einsum(
        "rhl,hlv->rhv", normal_lat, w_uv, preferred_element_type=jnp.float32
    ).astype(jnp.bfloat16).reshape(rows_here, heads_here * value_width)
    heads_all = exchange(
        heads_kernel,
        bf16((ctx_count,) + head_out.shape),
        [dma((2, chips))] * 2,
        head_out,
    )
    heads_all = (
        heads_all.reshape(ctx_count, exp_count, tok_here, -1)
        .transpose(1, 0, 2, 3)
        .reshape(exp_count * ctx_count * tok_here, -1)
    )
    head_partial = jnp.dot(heads_all, w_out, preferred_element_type=jnp.float32)
    group = ctx_count * tok_here
    hidden_all = exchange(
        hidden_kernel,
        bf16((ctx_count, exp_count, group, col_part)),
        [pltpu.VMEM((exp_count, group, col_part), jnp.bfloat16)]
        + [dma((exp_count,))] * 4
        + [dma((chips, exp_count))] * 4,
        head_partial.astype(jnp.bfloat16).reshape(exp_count, group, col_part),
        res_own.reshape(group, col_part),
    )
    tokens = exp_count * group
    hidden_rows = hidden_all.reshape(ctx_count, tokens, col_part).transpose(1, 0, 2)
    hidden_rows = hidden_rows.reshape(tokens, model_width)
    hidden = hidden_rows.astype(jnp.float32)
    mean_square = jnp.mean(hidden * hidden, axis=1, keepdims=True)
    normed = (hidden * lax.rsqrt(mean_square + NORM_EPS) * norm_gain).astype(jnp.bfloat16)
    affinity = jax.nn.sigmoid(jnp.dot(normed, router_weight, preferred_element_type=jnp.float32))
    expert_count = router_weight.shape[1]
    ids = ids_all.transpose(1, 0, 2, 3).reshape(tokens, -1)
    onehot = ids[:, :, None] == jnp.arange(expert_count, dtype=jnp.int32)[None, None, :]
    named = jnp.any(onehot, axis=1)
    chosen = jnp.where(named, affinity, 0.0)
    mixing = ROUTE_SCALE * chosen / jnp.sum(chosen, axis=1, keepdims=True)
    local_experts, _, hidden_units = w_gate.shape
    mine = lax.dynamic_slice_in_dim(mixing, exp_index * local_experts, local_experts, axis=1)
    acts = []
    for i in range(local_experts):
        gate = jnp.dot(normed, w_gate[i], preferred_element_type=jnp.float32)
        upward = jnp.dot(normed, w_up[i], preferred_element_type=jnp.float32)
        acts.append((jax.nn.silu(gate) * upward * mine[:, i : i + 1]).astype(jnp.bfloat16))
    acts = jnp.concatenate(acts, axis=1)
    down = w_down.reshape(local_experts * hidden_units, model_width)
    mixed = jnp.dot(acts, down, preferred_element_type=jnp.float32).astype(jnp.bfloat16)
    own_hidden = lax.dynamic_slice_in_dim(
        hidden_rows, (exp_index * ctx_count + ctx_index) * tok_here, tok_here, axis=0
    )
    block = (tok_here, model_width)
    return exchange(
        combine_kernel,
        bf16(block),
        [pltpu.VMEM((exp_count, chips) + block, jnp.bfloat16)] * 3
        + [pltpu.VMEM((exp_count,) + block, jnp.bfloat16)] * 2
        + [dma((exp_count, chips))] * 4
        + [dma((exp_count,))] * 2,
        mixed.reshape((exp_count, ctx_count) + block),
        own_hidden,
    )


def solution(mesh):
    return jax.shard_map(
        body,
        mesh=mesh,
        in_specs=(
            P("ctx", "exp", None),
            P("ctx", "exp"),
            P(None, "ctx"),
            P(None, "ctx"),
            P(),
            P("exp", None, None),
            P("exp", "ctx"),
            P(("ctx", "exp"), None),
            P(),
            P(),
            P(("ctx", "exp"), None),
            P("exp", None, "ctx"),
            P("exp", None, "ctx"),
            P("exp", "ctx", None),
        ),
        out_specs=P(("ctx", "exp"), None),
        check_vma=False,
    )
```

time: 270 us -> 139 us (0.51)
  waiting for transfers between devices: 153 us -> 0 us
  Pallas kernels: 0 us -> 85.8 us
  blocking collectives: 44.4 us -> 0 us
  between operations: 13.4 us -> 0.4 us
  starting transfers between devices: 9.06 us -> 0 us
  local copies, waits for them, and re-layouts: 14.2 us -> 18.4 us
  matrix products: 30.6 us -> 26.5 us
    unnamed x5 -> x0, waiting for transfers between devices: 108 us -> none
    pallas_call x0 -> x4, Pallas kernels: none -> 85.8 us  [exchange(): pl.pallas_call(kernel, out_shape=shapes, in_specs=[vmem] * len(operands),...]
    all_to_all x1 -> x0, blocking collectives: 26.9 us -> none  [body(): lax.all_to_all(send_rows.reshape(expert_count, CAP, model_width), 'exp',...]
    all_gather x1 -> x0, waiting for transfers between devices: 23.9 us -> none  [body(): portion = lax.all_gather(arrived, 'ctx', axis=1, tiled=True)]
    all_to_all x2 -> x0, waiting for transfers between devices: 20.6 us -> none  [the longest x1 17.2 us: body(): lax.all_to_all(going_back, 'exp', split_axis=0, concat_axis=2, tiled=True)]
    all_gather x2 -> x0, blocking collectives: 17.5 us -> none  [the longest x1 10.3 us: body(): portion = lax.all_gather(keys_here, 'ctx', axis=1, tiled=True)]
    all_to_all x2 -> x0, starting transfers between devices: 8.8 us -> none  [the longest x1 5.52 us: body(): lax.all_to_all(going_back, 'exp', split_axis=0, concat_axis=2, tiled=True)]
    reshape x3 -> x9, local copies, waits for them, and re-layouts: 0.73 us -> 7.35 us  [the longest x1 4.22 us: body(): mixed.reshape((exp_count, ctx_count) + block)]
  transfers between devices with their start and end apart: 5 -> 0, of which waited for: 5 -> 0; matrix products, arithmetic and copies ran while one was open for 1% -> 0% of each run, Pallas kernels for 0% -> 0%
where the time goes in v1:
time: 139 us; the launch traced here: 138 us
  Pallas kernels  85.8 us (62%)
  matrix products  26.5 us (19%)
  local copies, waits for them, and re-layouts  18.4 us (13%)
  other arithmetic  6.7 us (5%)
    pallas_call x4, Pallas kernels, exchange(): pl.pallas_call(kernel, out_shape=shapes, in_specs=[vmem] * len(operands),...  85.8 us
    dot_general x2, matrix products, body(): upward = jnp.dot(normed, w_up[i], preferred_element_type=jnp.float32)  8.73 us
    unnamed x43, local copies, waits for them, and re-layouts  6.38 us
    dot_general x2, matrix products, body(): gate = jnp.dot(normed, w_gate[i], preferred_element_type=jnp.float32)  5.47 us
    dot_general x1, matrix products, body(): head_partial = jnp.dot(heads_all, w_out, preferred_element_type=jnp.float32)  4.36 us
    reshape x1, local copies, waits for them, and re-layouts, body(): mixed.reshape((exp_count, ctx_count) + block)  4.22 us
    dot_general x1, matrix products, body(): jnp.dot(acts, down, preferred_element_type=jnp.float32).astype(jnp.bfloat16)  3.59 us

profile of v1, /device:TPU:0, one launch (start us, length us, event | category | flops | bytes accessed | tf_op | source)
XLA Modules:
  0.0 137.7 jit_solution(2937662491723786002)
XLA Ops:
  0.0 0.9 select_reduce_fusion
  0.9 0.7 select_reduce_fusion.1
  1.7 0.1 broadcast_compare_fusion
  1.8 1.4 mul.119
  3.1 1.7 %reshape.188 = bf16[512,64]{1,0:T(8,128)(2,1)} reshape(bf16[32,1024]{1,0:T(8,128)(2,1)} %param.15) | data formatting | bytes 131072 | tf_op jit(solution)/shard_map/reshape | solution.py:35
  4.8 0.1 broadcast_in_dim.62
  4.9 0.9 copy-done.3
  5.8 0.8 copy-done.4
  6.6 0.8 copy-done.5
  7.4 0.7 copy-done.6
  8.1 17.0 %shard_map.136 = (bf16[4,576,128]{2,1,0:T(8,128)(2,1)S(1)}, bf16[4,32,576]{2,1,0:T(8,128)(2,1)S(1)}, bf16[4,4,1792]{2,1,0:T(4,128)(2,1)S(1)}, s32[4,8,4,8]{3,2,1,0:T(4,128)S(1)}) custom-call(bf16[576,128]{1,0:T(8,128)(2,1)S(1)} %copy-done.3, bf16[32,576]{1,0:T(8,128)(2,1)S(1)} %bitcast.91, bf16[4,4,1792]{2,1,0:T(4,128)(2,1)S(1)} %bitcast.90, ...), custom_call_target="tpu_custom_call" | custom-call | tf_op jit(solution)/shard_map/pallas_call | solution.py:267
  25.1 0.1 copy_bitcast_fusion
  25.1 0.1 copy.26
  25.4 0.6 fusion.60
  26.0 1.6 %fusion.68 = f32[640,512]{0,1:T(8,128)S(1)} fusion(bf16[512,512]{1,0:T(8,128)(2,1)} %bitcast.112, bf16[576,512]{1,0:T(8,128)(2,1)S(1)} %copy_bitcast_fusion, bf16[576,128]{1,0:T(8,128)(2,1)S(1)} %bitcast.106), kind=kOutput, calls=%fused_computation.88 | convolution fusion | flops 336855040 | bytes 2572288 | tf_op jit(solution)/shard_map/dot_general | solution.py:29
  27.6 0.5 fusion.70
  28.1 0.4 fusion.35
  28.5 0.7 div.60
  29.2 0.8 copy.28
  30.0 1.5 %fusion.44 = bf16[16,4,8,128]{3,2,1,0:T(8,128)(2,1)} fusion(bf16[16,512,128]{2,1,0:T(8,128)(2,1)S(1)} %copy-done, bf16[32,16,640]{2,1,0:T(8,128)(2,1)S(1)} %bitcast.105, f32[32,16]{0,1:T(8,128)S(1)} %copy.28, bf16[576,512]{1,0:T(8,128)(2,1)S(1)} %copy_bitcast_fusion, bf16[576,128]{1,0:T(8,128)(2,1)S(1)} %bitcast.108), kind=kOutput, calls=%fused_computation.40 | convolution fusion | flops 404553728 | bytes 3622912 | tf_op jit(solution)/shard_map/rhl,hlv->rhv/dot_general | solution.py:337
  31.5 0.9 copy.47
  32.4 10.4 %shard_map.137 = bf16[4,32,2048]{2,1,0:T(8,128)(2,1)S(1)} custom-call(bf16[32,2048]{1,0:T(8,128)(2,1)S(1)} %bitcast.87), custom_call_target="tpu_custom_call" | custom-call | tf_op jit(solution)/shard_map/pallas_call | solution.py:267
  42.8 0.2 reshape.190
  43.0 0.2 copy.46
  43.3 0.1 reshape.191
  43.4 0.0 slice-start.4
  43.4 4.4 %convolution_convert_fusion.1 = bf16[128,1792]{1,0:T(8,128)(2,1)S(1)} fusion(bf16[128,2048]{1,0:T(8,128)(2,1)S(1)} %reshape.191, bf16[2048,1792]{1,0:T(8,128)(2,1)} %param.20), kind=kOutput, calls=%fused_computation.19 | convolution fusion | flops 939753472 | bytes 8323072 | tf_op jit(solution)/shard_map/dot_general | solution.py:351
  47.8 0.0 slice-start.5
  47.8 36.6 %shard_map.138 = bf16[4,8,16,1792]{3,2,1,0:T(8,128)(2,1)S(1)} custom-call(bf16[8,16,1792]{2,1,0:T(8,128)(2,1)S(1)} %bitcast.86, bf16[16,1792]{1,0:T(8,128)(2,1)S(1)} %reshape.193.res), custom_call_target="tpu_custom_call" | custom-call | tf_op jit(solution)/shard_map/pallas_call | solution.py:267
  84.4 2.4 %fusion.12 = f32[128]{0:T(128)S(1)} fusion(bf16[4,128,1792]{2,1,0:T(8,128)(2,1)S(1)} %bitcast.83), kind=kLoop, calls=%fused_computation.15 | loop fusion | flops 2752384 | bytes 1835520 | tf_op jit(solution)/shard_map/reduce_sum | solution.py:366
  86.7 1.6 %fusion.14 = bf16[128,4,1792]{2,1,0:T(4,128)(2,1)S(1)} fusion(f32[4,1792]{1,0:T(4,128)S(1)} %copy-done.8, f32[128]{0:T(128)S(1)} %add_rsqrt_fusion, bf16[4,128,1792]{2,1,0:T(8,128)(2,1)S(1)} %bitcast.84), kind=kLoop, calls=%fused_computation.17 | loop fusion | flops 3670016 | bytes 3699200 | tf_op jit(solution)/shard_map/convert_element_type | solution.py:367
  88.3 1.4 %copy.31 = bf16[4,128,1792]{2,0,1:T(4,128)(2,1)S(1)} copy(bf16[4,128,1792]{2,1,0:T(8,128)(2,1)S(1)} %bitcast.85) | data formatting | bytes 3670016 | tf_op jit(solution)/shard_map/reshape | solution.py:363
  89.8 0.2 copy.36
  90.0 0.0 slice-start.6
  90.0 0.2 copy.37
  90.3 0.4 copy-done.11
  90.7 0.1 copy-done.9
  90.8 0.7 fusion.71
  91.6 4.3 %fusion.2 = f32[128,512]{1,0:T(8,128)S(1)} fusion(bf16[128,7168]{1,0:T(8,128)(2,1)S(1)} %bitcast.100, bf16[2,7168,512]{2,1,0:T(8,128)(2,1)} %param.25), kind=kOutput, calls=%fused_computation.3 | convolution fusion | flops 939524096 | bytes 9437184 | tf_op jit(solution)/shard_map/dot_general | solution.py:379
  96.0 4.4 %fusion.38 = bf16[128,512]{1,0:T(8,128)(2,1)S(1)} fusion(bf16[128,7168]{1,0:T(8,128)(2,1)S(1)} %bitcast.101, bf16[2,7168,512]{2,1,0:T(8,128)(2,1)} %param.26, f32[128,512]{1,0:T(8,128)S(1)} %fusion.2, f32[128]{0:T(128)S(1)} %get-tuple-element.16), kind=kOutput, calls=%fused_computation.38 | convolution fusion | flops 939982848 | bytes 9568768 | tf_op jit(solution)/shard_map/dot_general | solution.py:380
  100.4 0.0 slice-start.2
  100.4 1.1 fusion.6
  101.5 4.4 %fusion.41 = bf16[128,512]{1,0:T(8,128)(2,1)S(1)} fusion(bf16[128,7168]{1,0:T(8,128)(2,1)S(1)} %bitcast.103, bf16[2,7168,512]{2,1,0:T(8,128)(2,1)} %param.26, f32[128,512]{1,0:T(8,128)S(1)} %fusion.6, f32[128]{0:T(128)S(1)} %get-tuple-element.15), kind=kOutput, calls=%fused_computation.39 | convolution fusion | flops 939982848 | bytes 9568768 | tf_op jit(solution)/shard_map/dot_general | solution.py:380
  106.0 3.6 %convolution_convert_fusion = bf16[128,7168]{1,0:T(8,128)(2,1)} fusion(bf16[1024,7168]{1,0:T(8,128)(2,1)S(1)} %bitcast.94, bf16[128,512]{1,0:T(8,128)(2,1)S(1)} %fusion.38, bf16[128,512]{1,0:T(8,128)(2,1)S(1)} %fusion.41), kind=kOutput, calls=%fused_computation | convolution fusion | flops 1880489984 | bytes 16777216 | tf_op jit(solution)/shard_map/dot_general | solution.py:384
  109.6 4.2 %reshape.197.y = bf16[8,4,4,7168]{3,2,1,0:T(4,128)(2,1)} reshape(bf16[128,7168]{1,0:T(8,128)(2,1)} %convolution_convert_fusion) | data formatting | bytes 3670016 | tf_op jit(solution)/shard_map/reshape | solution.py:396
  113.8 1.5 %copy-done.2 = bf16[8,4,4,7168]{3,2,1,0:T(4,128)(2,1)S(1)} copy-done((bf16[8,4,4,7168]{3,2,1,0:T(4,128)(2,1)S(1)}, bf16[8,4,4,7168]{3,2,1,0:T(4,128)(2,1)}, u32[]{:S(2)}) %copy-start.2) | copy-done | bytes 1835032
  115.3 21.8 %shard_map.139 = bf16[4,7168]{1,0:T(4,128)(2,1)S(1)} custom-call(bf16[8,4,4,7168]{3,2,1,0:T(4,128)(2,1)S(1)} %copy-done.2, bf16[4,7168]{1,0:T(4,128)(2,1)S(1)} %constant_dynamic-slice_fusion.hid), custom_call_target="tpu_custom_call" | custom-call | tf_op jit(solution)/shard_map/pallas_call | solution.py:267
  137.1 0.6 copy.49
  (43 shorter events, 0.3 us)
Async XLA Ops:
  0.0 30.0 %copy-start = (bf16[16,512,128]{2,1,0:T(8,128)(2,1)S(1)}, bf16[16,512,128]{2,1,0:T(8,128)(2,1)}, u32[]{:S(2)}) copy-start(bf16[16,512,128]{2,1,0:T(8,128)(2,1)} %param.19) | copy-start | bytes 6291460
  4.9 0.9 copy-start.3
  5.8 0.8 copy-start.4
  6.6 0.8 copy-start.5
  7.4 0.7 copy-start.6
  25.3 2.3 %copy-start.7 = (bf16[512,64]{1,0:T(8,128)(2,1)S(1)}, bf16[512,64]{1,0:T(8,128)(2,1)}, u32[]{:S(2)}) copy-start(bf16[512,64]{1,0:T(8,128)(2,1)} %reshape.188) | copy-start | bytes 196612
  43.4 56.9 %slice-start.4 = ((s8[14680064]{0:T(1024)(128)(4,1)}), s8[2097152]{0:T(1024)(128)(4,1)S(1)}, s32[]{:S(2)}) async-start(s8[14680064]{0:T(1024)(128)(4,1)} %bitcast.110), calls=%async_computation.4 | async-start | bytes 4194304
  47.8 39.0 %copy-start.8 = (f32[4,1792]{1,0:T(4,128)S(1)}, f32[4,1792]{1,0:T(4,128)}, u32[]{:S(2)}) copy-start(f32[4,1792]{1,0:T(4,128)} %mul.119) | copy-start | bytes 86020
  47.8 52.6 %slice-start.5 = ((s8[14680064]{0:T(1024)(128)(4,1)}), s8[4194304]{0:T(1024)(128)(4,1)S(1)}, s32[]{:S(2)}) async-start(s8[14680064]{0:T(1024)(128)(4,1)} %bitcast.110), calls=%async_computation.5 | async-start | bytes 8388608
  89.7 0.9 copy-start.11
  90.0 0.8 copy-start.9
  90.0 0.8 copy-start.10
  90.0 10.3 %slice-start.6 = ((s8[14680064]{0:T(1024)(128)(4,1)}), s8[4194304]{0:T(1024)(128)(4,1)S(1)}, s32[]{:S(2)}) async-start(s8[14680064]{0:T(1024)(128)(4,1)} %bitcast.110), calls=%async_computation.6 | async-start | bytes 8388608
  91.6 8.8 %slice-start.7 = ((s8[14680064]{0:T(1024)(128)(4,1)}), s8[4194304]{0:T(1024)(128)(4,1)S(1)}, s32[]{:S(2)}) async-start(s8[14680064]{0:T(1024)(128)(4,1)} %bitcast.110), calls=%async_computation.7 | async-start | bytes 8388608
  95.9 10.0 %slice-start = ((s8[14680064]{0:T(1024)(128)(4,1)}), s8[4194304]{0:T(1024)(128)(4,1)S(1)}, s32[]{:S(2)}) async-start(s8[14680064]{0:T(1024)(128)(4,1)} %bitcast.92), calls=%async_computation | async-start | bytes 8388608
  95.9 10.0 %slice-start.1 = ((s8[14680064]{0:T(1024)(128)(4,1)}), s8[4194304]{0:T(1024)(128)(4,1)S(1)}, s32[]{:S(2)}) async-start(s8[14680064]{0:T(1024)(128)(4,1)} %bitcast.92), calls=%async_computation.1 | async-start | bytes 8388608
  100.4 5.5 %slice-start.2 = ((s8[14680064]{0:T(1024)(128)(4,1)}), s8[4194304]{0:T(1024)(128)(4,1)S(1)}, s32[]{:S(2)}) async-start(s8[14680064]{0:T(1024)(128)(4,1)} %bitcast.92), calls=%async_computation.2 | async-start | bytes 8388608
  101.5 4.4 %slice-start.3 = ((s8[14680064]{0:T(1024)(128)(4,1)}), s8[2097152]{0:T(1024)(128)(4,1)S(1)}, s32[]{:S(2)}) async-start(s8[14680064]{0:T(1024)(128)(4,1)} %bitcast.92), calls=%async_computation.3 | async-start | bytes 4194304
  109.5 28.2 %copy-start.1 = (bf16[16,512,128]{2,1,0:T(8,128)(2,1)S(1)}, bf16[16,512,128]{2,1,0:T(8,128)(2,1)}, u32[]{:S(2)}) copy-start(bf16[16,512,128]{2,1,0:T(8,128)(2,1)} %param.19) | copy-start | bytes 6291460
  113.8 1.5 %copy-start.2 = (bf16[8,4,4,7168]{3,2,1,0:T(4,128)(2,1)S(1)}, bf16[8,4,4,7168]{3,2,1,0:T(4,128)(2,1)}, u32[]{:S(2)}) copy-start(bf16[8,4,4,7168]{3,2,1,0:T(4,128)(2,1)} %reshape.197.y) | copy-start | bytes 5505028

commit v2 on v1

--- a/solution.py
+++ b/solution.py
@@ -9,7 +9,8 @@
 from jax.sharding import PartitionSpec as P
 
 QKD = 192
-VMEM_BYTES = 48 * 1024 * 1024
+VMEM_BYTES = 56 * 1024 * 1024
+SPARE_BYTES = 2 * 1024 * 1024
 
 ROUTE_SCALE = 2.5
 NORM_EPS = 1e-06
@@ -65,6 +66,26 @@
     ctx_count, exp_count = lax.axis_size("ctx"), lax.axis_size("exp")
     ctx, exp = lax.axis_index("ctx"), lax.axis_index("exp")
     return ctx_count // 2, exp_count, ctx, exp, ctx // 2, ctx % 2
+
+
+def greet(over_exp):
+    ctx_count, exp_count = lax.axis_size("ctx"), lax.axis_size("exp")
+    ctx, exp = lax.axis_index("ctx"), lax.axis_index("exp")
+    barrier = pltpu.get_barrier_semaphore()
+    peers = [((ctx + k) % ctx_count, exp) for k in range(1, ctx_count)]
+    if over_exp:
+        peers += [(ctx, (exp + k) % exp_count) for k in range(1, exp_count)]
+    for peer in peers:
+        pl.semaphore_signal(
+            barrier, inc=1, device_id=peer, device_id_type=pl.DeviceIdType.MESH
+        )
+    pl.semaphore_wait(barrier, len(peers))
+
+
+def column_block(rows, wide, ctx, exp, width):
+    if not wide:
+        return rows.at[ctx, exp]
+    return rows.at[exp, :, pl.ds(pl.multiple_of(ctx * width, 128), width)]
 
 
 def start_gather(src, out, send, recv):
@@ -102,6 +123,7 @@
 ):
     chips, exp_count, ctx, exp, chip, core = place()
     ctx_count = 2 * chips
+    greet(True)
     id_flights = []
     for k in range(1, exp_count):
         copy = remote(
@@ -141,16 +163,20 @@
 
 def heads_kernel(src, out, send, recv):
     _, _, ctx, _, _, _ = place()
+    greet(False)
     flights = start_gather(src, out, send, recv)
     out[ctx] = src[...]
     finish_gather(out, flights, send, recv)
 
 
 def hidden_kernel(
-    part, res, out, landed, a_send, a_recv, b_send, b_recv, x_send, x_recv, f_send, f_recv
+    wide, part, res, out, landed, a_send, a_recv, b_send, b_recv, x_send, x_recv, f_send, f_recv
 ):
     chips, exp_count, ctx, exp, chip, core = place()
     partner = ctx + 1 - 2 * core
+    width = part.shape[2]
+    place_of = lambda c, e: column_block(out, wide, c, e, width)
+    greet(True)
     first = []
     for k in range(1, exp_count):
         peer = (exp + k) % exp_count
@@ -161,13 +187,14 @@
     for k in range(1, exp_count):
         first[k - 1].wait_recv()
         total = total + landed[k].astype(jnp.float32)
-    out[ctx, exp] = (res[...].astype(jnp.float32) + total).astype(jnp.bfloat16)
+    own = place_of(ctx, exp)
+    own[...] = (res[...].astype(jnp.float32) + total).astype(jnp.bfloat16)
     pending = []
     spread = [None]
     for k in range(1, exp_count):
         copy = remote(
-            out.at[ctx, exp],
-            out.at[ctx, exp],
+            own,
+            own,
             b_send.at[k],
             b_recv.at[k],
             (ctx, (exp + k) % exp_count),
@@ -178,7 +205,7 @@
         if k > 0:
             spread[k].wait_recv()
         source = (exp + exp_count - k) % exp_count
-        block = out.at[ctx, source]
+        block = place_of(ctx, source)
         row = []
         for p in range(chips):
             peer = partner if p == 0 else (chip + p) % chips * 2 + core
@@ -192,7 +219,7 @@
         for p in range(1, chips):
             pending[k][p].wait_recv()
             origin = (chip + chips - p) % chips * 2 + core
-            block = out.at[origin, source]
+            block = place_of(origin, source)
             copy = remote(block, block, f_send.at[p, k], f_recv.at[p, k], (partner, exp))
             copy.start()
             last.append(copy)
@@ -205,11 +232,14 @@
 
 
 def combine_kernel(
-    y, hid, out, pair, cross_out, cross_in, home_out, home_in,
-    p_send, p_recv, x_send, x_recv, e_send, e_recv,
+    wide, y, hid, out, pair, cross_out, cross_in, home_out, home_in, final,
+    p_send, p_recv, x_send, x_recv, e_send, e_recv, o_send, o_recv,
 ):
     chips, exp_count, ctx, exp, chip, core = place()
     partner = ctx + 1 - 2 * core
+    ctx_count, tok, width = out.shape
+    part_of = lambda c, e: column_block(y, wide, c, e, width)
+    greet(True)
     order = list(range(1, exp_count)) + [0]
     halves, crossing, homing = {}, {}, {}
     for k in order:
@@ -217,7 +247,11 @@
         for j in list(range(1, chips)) + [0]:
             theirs = (chip + j) % chips * 2 + 1 - core
             copy = remote(
-                y.at[dest, theirs], pair.at[k, j], p_send.at[k, j], p_recv.at[k, j], (partner, exp)
+                part_of(theirs, dest),
+                pair.at[k, j],
+                p_send.at[k, j],
+                p_recv.at[k, j],
+                (partner, exp),
             )
             copy.start()
             halves[k, j] = copy
@@ -226,7 +260,7 @@
         for j in range(1, chips):
             owner = (chip + j) % chips * 2 + core
             halves[k, j].wait_recv()
-            both = y[dest, owner].astype(jnp.float32) + pair[k, j].astype(jnp.float32)
+            both = part_of(owner, dest)[...].astype(jnp.float32) + pair[k, j].astype(jnp.float32)
             cross_out[k, j] = both.astype(jnp.bfloat16)
             copy = remote(
                 cross_out.at[k, j],
@@ -241,7 +275,7 @@
     for k in order:
         dest = (exp + k) % exp_count
         halves[k, 0].wait_recv()
-        both = y[dest, ctx].astype(jnp.float32) + pair[k, 0].astype(jnp.float32)
+        both = part_of(ctx, dest)[...].astype(jnp.float32) + pair[k, 0].astype(jnp.float32)
         for j in range(1, chips):
             crossing[k, j].wait_recv()
             both = both + cross_in[k, j].astype(jnp.float32)
@@ -257,13 +291,26 @@
     for k in range(1, exp_count):
         homing[k].wait_recv()
         total = total + home_in[k].astype(jnp.float32)
-    out[...] = total.astype(jnp.bfloat16)
+    for c in range(ctx_count):
+        final[c] = total[c * tok : (c + 1) * tok].astype(jnp.bfloat16)
+    last = []
+    for k in range(1, ctx_count):
+        peer = (ctx + k) % ctx_count
+        copy = remote(final.at[peer], out.at[ctx], o_send.at[k], o_recv.at[k], (peer, exp))
+        copy.start()
+        last.append(copy)
+    out[ctx] = final[ctx]
+    for copy in last:
+        copy.wait()
     for copy in list(halves.values()) + list(crossing.values()) + list(homing.values()):
         copy.wait_send()
 
 
-def exchange(kernel, shapes, scratch, *operands):
+def exchange(number, kernel, shapes, scratch, *operands):
     vmem = pl.BlockSpec(memory_space=pltpu.VMEM)
+    held = jax.tree.leaves(shapes) + list(operands)
+    held += [s for s in scratch if s.dtype == jnp.bfloat16]
+    need = sum(2 * math.prod(h.shape) * h.dtype.itemsize for h in held) + SPARE_BYTES
     return pl.pallas_call(
         kernel,
         out_shape=shapes,
@@ -271,7 +318,7 @@
         out_specs=jax.tree.map(lambda _: vmem, shapes),
         scratch_shapes=scratch,
         compiler_params=pltpu.CompilerParams(
-            has_side_effects=True, vmem_limit_bytes=VMEM_BYTES
+            collective_id=number, has_side_effects=True, vmem_limit_bytes=min(need, VMEM_BYTES)
         ),
     )(*operands)
 
@@ -308,6 +355,7 @@
 
     res_cols = residual.reshape(tok_here, ctx_count, col_part).transpose(1, 0, 2)
     cache_all, fresh_all, res_own, ids_all = exchange(
+        0,
         inputs_kernel,
         (
             bf16((ctx_count, key_width, cache_len)),
@@ -338,6 +386,7 @@
         "rhl,hlv->rhv", normal_lat, w_uv, preferred_element_type=jnp.float32
     ).astype(jnp.bfloat16).reshape(rows_here, heads_here * value_width)
     heads_all = exchange(
+        1,
         heads_kernel,
         bf16((ctx_count,) + head_out.shape),
         [dma((2, chips))] * 2,
@@ -350,18 +399,23 @@
     )
     head_partial = jnp.dot(heads_all, w_out, preferred_element_type=jnp.float32)
     group = ctx_count * tok_here
+    wide = col_part % 128 == 0
+    tokens = exp_count * group
+    stripes = (exp_count, group, model_width)
+    blocks = (ctx_count, exp_count, group, col_part)
     hidden_all = exchange(
-        hidden_kernel,
-        bf16((ctx_count, exp_count, group, col_part)),
+        2,
+        functools.partial(hidden_kernel, wide),
+        bf16(stripes if wide else blocks),
         [pltpu.VMEM((exp_count, group, col_part), jnp.bfloat16)]
         + [dma((exp_count,))] * 4
         + [dma((chips, exp_count))] * 4,
         head_partial.astype(jnp.bfloat16).reshape(exp_count, group, col_part),
         res_own.reshape(group, col_part),
     )
-    tokens = exp_count * group
-    hidden_rows = hidden_all.reshape(ctx_count, tokens, col_part).transpose(1, 0, 2)
-    hidden_rows = hidden_rows.reshape(tokens, model_width)
+    if not wide:
+        hidden_all = hidden_all.transpose(1, 2, 0, 3)
+    hidden_rows = hidden_all.reshape(tokens, model_width)
     hidden = hidden_rows.astype(jnp.float32)
     mean_square = jnp.mean(hidden * hidden, axis=1, keepdims=True)
     normed = (hidden * lax.rsqrt(mean_square + NORM_EPS) * norm_gain).astype(jnp.bfloat16)
@@ -382,20 +436,27 @@
     acts = jnp.concatenate(acts, axis=1)
     down = w_down.reshape(local_experts * hidden_units, model_width)
     mixed = jnp.dot(acts, down, preferred_element_type=jnp.float32).astype(jnp.bfloat16)
-    own_hidden = lax.dynamic_slice_in_dim(
-        hidden_rows, (exp_index * ctx_count + ctx_index) * tok_here, tok_here, axis=0
-    )
-    block = (tok_here, model_width)
-    return exchange(
-        combine_kernel,
-        bf16(block),
+    own_hidden = lax.dynamic_slice(
+        hidden_rows, (exp_index * group, ctx_index * col_part), (group, col_part)
+    )
+    mixed = mixed.reshape(stripes)
+    if not wide:
+        mixed = mixed.reshape(exp_count, group, ctx_count, col_part).transpose(2, 0, 1, 3)
+    block = (group, col_part)
+    owned = exchange(
+        3,
+        functools.partial(combine_kernel, wide),
+        bf16((ctx_count, tok_here, col_part)),
         [pltpu.VMEM((exp_count, chips) + block, jnp.bfloat16)] * 3
         + [pltpu.VMEM((exp_count,) + block, jnp.bfloat16)] * 2
+        + [pltpu.VMEM((ctx_count, tok_here, col_part), jnp.bfloat16)]
         + [dma((exp_count, chips))] * 4
-        + [dma((exp_count,))] * 2,
-        mixed.reshape((exp_count, ctx_count) + block),
+        + [dma((exp_count,))] * 2
+        + [dma((ctx_count,))] * 2,
+        mixed,
         own_hidden,
     )
+    return owned.transpose(1, 0, 2).reshape(tok_here, model_width)
 
 
 def solution(mesh):

time: 139 us -> 118 us (0.85)
  Pallas kernels: 85.8 us -> 76.3 us
  local copies, waits for them, and re-layouts: 18.4 us -> 8.98 us
  other arithmetic: 6.7 us -> 3.7 us
  matrix products: 26.5 us -> 27.9 us
    pallas_call x4, Pallas kernels: 85.8 us -> 76.3 us  [exchange(): pl.pallas_call(kernel, out_shape=shapes, in_specs=[vmem] * len(operands),...]
    reshape x2 -> x0, local copies, waits for them, and re-layouts: 5.64 us -> none  [the longest x1 4.22 us: body(): mixed.reshape((exp_count, ctx_count) + block)]
    dot_general x2, matrix products: 5.47 us -> 8.56 us  [body(): gate = jnp.dot(normed, w_gate[i], preferred_element_type=jnp.float32)]
    unnamed x43 -> x29, local copies, waits for them, and re-layouts: 6.38 us -> 3.87 us
    reduce_sum x1, other arithmetic: 2.37 us -> 0.43 us  [body(): mean_square = jnp.mean(hidden * hidden, axis=1, keepdims=True)]
    dot_general x1, matrix products: 3.59 us -> 2.08 us  [body(): jnp.dot(acts, down, preferred_element_type=jnp.float32).astype(jnp.bfloat16)]
where the time goes in v2:
time: 118 us; the launch traced here: 117 us
  Pallas kernels  76.3 us (65%)
  matrix products  27.9 us (24%)
  local copies, waits for them, and re-layouts  8.98 us (8%)
  other arithmetic  3.7 us (3%)
    pallas_call x4, Pallas kernels, exchange(): pl.pallas_call(kernel, out_shape=shapes, in_specs=[vmem] * len(operands),...  76.3 us
    dot_general x2, matrix products, body(): upward = jnp.dot(normed, w_up[i], preferred_element_type=jnp.float32)  8.73 us
    dot_general x2, matrix products, body(): gate = jnp.dot(normed, w_gate[i], preferred_element_type=jnp.float32)  8.56 us
    dot_general x1, matrix products, body(): head_partial = jnp.dot(heads_all, w_out, preferred_element_type=jnp.float32)  4.21 us
    unnamed x29, local copies, waits for them, and re-layouts  3.87 us

profile of v2, /device:TPU:0, one launch (start us, length us, event | category | flops | bytes accessed | tf_op | source)
XLA Modules:
  0.0 117.3 jit_solution(9574012158730810391)
XLA Ops:
  0.0 0.9 select_reduce_fusion
  0.9 0.7 select_reduce_fusion.1
  1.7 0.1 broadcast_compare_fusion
  1.8 1.7 %reshape.197 = bf16[512,64]{1,0:T(8,128)(2,1)} reshape(bf16[32,1024]{1,0:T(8,128)(2,1)} %param.15) | data formatting | bytes 131072 | tf_op jit(solution)/shard_map/reshape | solution.py:36
  3.4 0.1 broadcast_in_dim.62
  3.5 0.0 copy-start.2
  3.5 0.9 copy-done.2
  4.4 0.8 copy-done.3
  5.2 0.8 copy-done.4
  6.0 0.7 copy-done.5
  6.7 14.7 %shard_map.136 = (bf16[4,576,128]{2,1,0:T(8,128)(2,1)S(1)}, bf16[4,32,576]{2,1,0:T(8,128)(2,1)S(1)}, bf16[4,4,1792]{2,1,0:T(4,128)(2,1)S(1)}, s32[4,8,4,8]{3,2,1,0:T(4,128)S(1)}) custom-call(bf16[576,128]{1,0:T(8,128)(2,1)S(1)} %copy-done.2, bf16[32,576]{1,0:T(8,128)(2,1)S(1)} %bitcast.90, bf16[4,4,1792]{2,1,0:T(4,128)(2,1)S(1)} %bitcast.89, ...), custom_call_target="tpu_custom_call" | custom-call | tf_op jit(solution)/shard_map/pallas_call | solution.py:314
  21.4 0.1 copy_bitcast_fusion
  21.5 0.1 copy.24
  21.8 0.6 fusion.60
  22.4 1.6 %fusion.68 = f32[640,512]{0,1:T(8,128)S(1)} fusion(bf16[512,512]{1,0:T(8,128)(2,1)} %bitcast.105, bf16[576,512]{1,0:T(8,128)(2,1)S(1)} %copy_bitcast_fusion, bf16[576,128]{1,0:T(8,128)(2,1)S(1)} %bitcast.101), kind=kOutput, calls=%fused_computation.87 | convolution fusion | flops 336855040 | bytes 2572288 | tf_op jit(solution)/shard_map/dot_general | solution.py:30
  24.0 0.5 fusion.70
  24.5 0.4 fusion.35
  24.9 0.7 div.60
  25.6 0.8 copy.26
  26.3 1.5 %fusion.44 = bf16[16,4,8,128]{3,2,1,0:T(8,128)(2,1)} fusion(bf16[16,512,128]{2,1,0:T(8,128)(2,1)S(1)} %copy-done, bf16[32,16,640]{2,1,0:T(8,128)(2,1)S(1)} %bitcast.100, f32[32,16]{0,1:T(8,128)S(1)} %copy.26, bf16[576,512]{1,0:T(8,128)(2,1)S(1)} %copy_bitcast_fusion, bf16[576,128]{1,0:T(8,128)(2,1)S(1)} %bitcast.103), kind=kOutput, calls=%fused_computation.40 | convolution fusion | flops 404553728 | bytes 3622912 | tf_op jit(solution)/shard_map/rhl,hlv->rhv/dot_general | solution.py:385
  27.9 0.9 copy.40
  28.8 6.9 %shard_map.137 = bf16[4,32,2048]{2,1,0:T(8,128)(2,1)S(1)} custom-call(bf16[32,2048]{1,0:T(8,128)(2,1)S(1)} %bitcast.85), custom_call_target="tpu_custom_call" | custom-call | tf_op jit(solution)/shard_map/pallas_call | solution.py:314
  35.7 0.2 reshape.199
  35.9 0.2 copy.39
  36.2 0.1 reshape.200
  36.3 4.2 %convolution_convert_fusion.1 = bf16[128,1792]{1,0:T(8,128)(2,1)S(1)} fusion(bf16[128,2048]{1,0:T(8,128)(2,1)S(1)} %reshape.200, bf16[2048,1792]{1,0:T(8,128)(2,1)} %param.20), kind=kOutput, calls=%fused_computation.19 | convolution fusion | flops 939753472 | bytes 8323072 | tf_op jit(solution)/shard_map/dot_general | solution.py:400
  40.5 0.0 copy-start.7
  40.5 0.0 copy-start.9
  40.5 29.3 %shard_map.138 = bf16[8,16,7168]{2,1,0:T(8,128)(2,1)S(1)} custom-call(bf16[8,16,1792]{2,1,0:T(8,128)(2,1)S(1)} %bitcast.84, bf16[16,1792]{1,0:T(8,128)(2,1)S(1)} %reshape.202.res), custom_call_target="tpu_custom_call" | custom-call | tf_op jit(solution)/shard_map/pallas_call | solution.py:314
  69.9 0.4 fusion.12
  70.3 0.1 rsqrt.13
  70.4 0.0 copy-done.7
  70.4 0.0 copy-done.8
  70.4 0.0 copy-done.9
  70.5 0.7 fusion.71
  71.2 0.5 fusion.14
  71.7 4.2 %fusion.2 = f32[128,512]{1,0:T(8,128)S(1)} fusion(bf16[128,7168]{1,0:T(8,128)(2,1)S(1)} %bitcast.95, bf16[2,7168,512]{2,1,0:T(8,128)(2,1)} %param.25), kind=kOutput, calls=%fused_computation.3 | convolution fusion | flops 939524096 | bytes 9437184 | tf_op jit(solution)/shard_map/dot_general | solution.py:433
  75.9 0.0 slice-start
  76.0 0.0 slice-start.1
  76.0 4.4 %fusion.38 = bf16[128,512]{1,0:T(8,128)(2,1)S(1)} fusion(bf16[128,7168]{1,0:T(8,128)(2,1)S(1)} %bitcast.96, bf16[2,7168,512]{2,1,0:T(8,128)(2,1)} %param.26, f32[128,512]{1,0:T(8,128)S(1)} %fusion.2, f32[128]{0:T(128)S(1)} %get-tuple-element.16), kind=kOutput, calls=%fused_computation.38 | convolution fusion | flops 939982848 | bytes 9568768 | tf_op jit(solution)/shard_map/dot_general | solution.py:434
  80.3 0.0 slice-start.2
  80.3 4.4 %fusion.6 = f32[128,512]{1,0:T(8,128)S(1)} fusion(bf16[128,7168]{1,0:T(8,128)(2,1)S(1)} %bitcast.97, bf16[2,7168,512]{2,1,0:T(8,128)(2,1)} %param.25), kind=kOutput, calls=%fused_computation.7 | convolution fusion | flops 939524096 | bytes 9437184 | tf_op jit(solution)/shard_map/dot_general | solution.py:433
  84.7 0.0 slice-start.3
  84.7 4.4 %fusion.41 = bf16[128,512]{1,0:T(8,128)(2,1)S(1)} fusion(bf16[128,7168]{1,0:T(8,128)(2,1)S(1)} %bitcast.98, bf16[2,7168,512]{2,1,0:T(8,128)(2,1)} %param.26, f32[128,512]{1,0:T(8,128)S(1)} %fusion.6, f32[128]{0:T(128)S(1)} %get-tuple-element.15), kind=kOutput, calls=%fused_computation.39 | convolution fusion | flops 939982848 | bytes 9568768 | tf_op jit(solution)/shard_map/dot_general | solution.py:434
  89.1 0.0 copy-start.1
  89.2 2.1 %convolution_convert_fusion = bf16[128,7168]{1,0:T(8,128)(2,1)S(1)} fusion(bf16[1024,7168]{1,0:T(8,128)(2,1)S(1)} %bitcast.93, bf16[128,512]{1,0:T(8,128)(2,1)S(1)} %fusion.38, bf16[128,512]{1,0:T(8,128)(2,1)S(1)} %fusion.41), kind=kOutput, calls=%fused_computation | convolution fusion | flops 1880489984 | bytes 16777216 | tf_op jit(solution)/shard_map/dot_general | solution.py:438
  91.2 25.4 %shard_map.139 = bf16[4,4,1792]{2,1,0:T(4,128)(2,1)S(1)} custom-call(bf16[8,16,7168]{2,1,0:T(8,128)(2,1)S(1)} %bitcast.83, bf16[16,1792]{1,0:T(8,128)(2,1)S(1)} %dynamic_slice.7.hid), custom_call_target="tpu_custom_call" | custom-call | tf_op jit(solution)/shard_map/pallas_call | solution.py:314
  116.6 0.6 copy.42
  (26 shorter events, 0.2 us)
Async XLA Ops:
  0.0 26.3 %copy-start = (bf16[16,512,128]{2,1,0:T(8,128)(2,1)S(1)}, bf16[16,512,128]{2,1,0:T(8,128)(2,1)}, u32[]{:S(2)}) copy-start(bf16[16,512,128]{2,1,0:T(8,128)(2,1)} %param.19) | copy-start | bytes 6291460
  3.5 0.9 copy-start.2
  4.4 0.8 copy-start.3
  5.2 0.8 copy-start.4
  6.0 0.7 copy-start.5
  21.7 2.3 %copy-start.6 = (bf16[512,64]{1,0:T(8,128)(2,1)S(1)}, bf16[512,64]{1,0:T(8,128)(2,1)}, u32[]{:S(2)}) copy-start(bf16[512,64]{1,0:T(8,128)(2,1)} %reshape.197) | copy-start | bytes 196612
  40.5 29.9 %copy-start.7 = (f32[7168]{0:T(1024)S(1)}, f32[7168]{0:T(1024)}, u32[]{:S(2)}) copy-start(f32[7168]{0:T(1024)} %param.22) | copy-start | bytes 86020
  40.5 29.9 %copy-start.8 = (pred[128,16]{0,1:T(8,128)(4,1)S(1)}, pred[128,16]{0,1:T(8,128)(4,1)}, u32[]{:S(2)}) copy-start(pred[128,16]{0,1:T(8,128)(4,1)} %fusion.60) | copy-start | bytes 6148
  40.5 29.9 %copy-start.9 = (bf16[7168,16]{0,1:T(8,128)(2,1)S(1)}, bf16[7168,16]{0,1:T(8,128)(2,1)}, u32[]{:S(2)}) copy-start(bf16[7168,16]{0,1:T(8,128)(2,1)} %param.23) | copy-start | bytes 688132
  75.9 13.2 %slice-start = ((s8[14680064]{0:T(1024)(128)(4,1)}), s8[4194304]{0:T(1024)(128)(4,1)S(1)}, s32[]{:S(2)}) async-start(s8[14680064]{0:T(1024)(128)(4,1)} %bitcast.91), calls=%async_computation | async-start | bytes 8388608
  76.0 13.2 %slice-start.1 = ((s8[14680064]{0:T(1024)(128)(4,1)}), s8[4194304]{0:T(1024)(128)(4,1)S(1)}, s32[]{:S(2)}) async-start(s8[14680064]{0:T(1024)(128)(4,1)} %bitcast.91), calls=%async_computation.1 | async-start | bytes 8388608
  80.3 8.8 %slice-start.2 = ((s8[14680064]{0:T(1024)(128)(4,1)}), s8[4194304]{0:T(1024)(128)(4,1)S(1)}, s32[]{:S(2)}) async-start(s8[14680064]{0:T(1024)(128)(4,1)} %bitcast.91), calls=%async_computation.2 | async-start | bytes 8388608
  84.7 4.4 %slice-start.3 = ((s8[14680064]{0:T(1024)(128)(4,1)}), s8[2097152]{0:T(1024)(128)(4,1)S(1)}, s32[]{:S(2)}) async-start(s8[14680064]{0:T(1024)(128)(4,1)} %bitcast.91), calls=%async_computation.3 | async-start | bytes 4194304
  89.1 28.1 %copy-start.1 = (bf16[16,512,128]{2,1,0:T(8,128)(2,1)S(1)}, bf16[16,512,128]{2,1,0:T(8,128)(2,1)}, u32[]{:S(2)}) copy-start(bf16[16,512,128]{2,1,0:T(8,128)(2,1)} %param.19) | copy-start | bytes 6291460
